TPU v7x, 32 devices: a whole 2x2x4 slice. The times are simulated.
32 devices in a mesh: section: 8 (over z, x), lat: 4 (over y, core).
Axes of the slice: x: 2, y: 2, z: 4, core: 2. Of those that a mesh axis runs over, the one named last changes fastest.
Arguments:
- activations: bfloat16 [8, 2, 64, 8192], P('section', None, None, 'lat'), may hold values from 0.5 to 3
- block_mask: int32 [8, 2, 64], P('section', None, 'lat'), may hold values 0 or 1
- enc_weight: bfloat16 [8, 2304, 8192], P('section', None, 'lat'), may hold values from -0.015625 to 0.015625
- dec_own: bfloat16 [8, 8192, 2304], P('section', 'lat'), may hold values from -0.125 to 0.125
- dec_next: bfloat16 [8, 8192, 2304], P('section', 'lat'), may hold values from -0.125 to 0.125
- grad_seed: float32 [2, 64, 2304], P(None, 'lat'), may hold values from -6 to 6
Outputs:
- residual_grads: float32 [8, 2, 64, 2304], P('section', None, 'lat')
- attribution: bfloat16 [8, 2, 64, 8192], P('section', None, None, 'lat')
All inputs are finite; a program needn't handle non-finite values. No bound on the sum of `block_mask` on one device may be relied on, other than what follows from the above.
Results may differ from a plain program's by a relative error of at most 0.01.
Values may be sent and summed in bfloat16 or wider, within the bound.
A program may use at most 64 MiB of HBM per device.

v0:
```python
import jax
import jax.numpy as jnp
from jax import lax
from jax.sharding import PartitionSpec as P


def shifted(block, axis, distance):
    devices = range(lax.axis_size(axis))
    route = [(i - distance, i) for i in devices if i - distance in devices]
    return lax.ppermute(block, axis, route)


def local(activations, block_mask, enc_weight, dec_own, dec_next, grad_seed):
    section_count = lax.axis_size("section")
    section_index = lax.axis_index("section")
    batch_count = activations.shape[1]
    micro_rows = activations.shape[2]
    latent_count = activations.shape[3]
    owned_rows = grad_seed.shape[1]
    model_width = grad_seed.shape[2]
    block_width = latent_count // block_mask.shape[2]
    own_weight = dec_own[0]
    next_weight = dec_next[0]
    encoder = enc_weight[0]
    above_init = jnp.zeros((micro_rows, model_width), jnp.bfloat16)
    grads_init = jnp.zeros((batch_count, owned_rows, model_width), jnp.float32)
    attrib_init = jnp.zeros((batch_count, micro_rows, latent_count), jnp.bfloat16)
    lower_init = jnp.zeros((owned_rows, model_width), jnp.float32)

    def advance(moment, state_now):
        sent_lower, sent_above, grads_acc, attrib_acc = state_now
        got_lower = shifted(sent_lower, "section", -1)
        batch_pos = moment - (section_count - 1 - section_index)
        is_valid = jnp.logical_and(batch_pos >= 0, batch_pos < batch_count)
        batch_index = jnp.clip(batch_pos, 0, batch_count - 1)
        seed_rows = lax.dynamic_index_in_dim(grad_seed, batch_index, 0, keepdims=False)
        grad_upper = jnp.where(section_index == section_count - 1, seed_rows, got_lower)
        upper_bf = grad_upper.astype(jnp.bfloat16)
        got_above = shifted(sent_above, "section", -1)
        full_upper = lax.all_gather(upper_bf, "lat", axis=0, tiled=True)
        grad_act = jnp.dot(full_upper, own_weight.T, preferred_element_type=jnp.float32)
        grad_act = grad_act + jnp.dot(got_above, next_weight.T, preferred_element_type=jnp.float32)
        mask_row = lax.dynamic_index_in_dim(block_mask[0], batch_index, 0, keepdims=False)
        gate_full = jnp.repeat(mask_row.astype(jnp.float32), block_width)
        act_rows = lax.dynamic_index_in_dim(activations[0], batch_index, 0, keepdims=False)
        active = act_rows.astype(jnp.float32) * gate_full[None, :]
        attrib_now = (active * grad_act).astype(jnp.bfloat16)
        grad_latent = (grad_act * gate_full[None, :]).astype(jnp.bfloat16)
        owned_sum = lax.psum_scatter(
            jnp.dot(grad_latent, encoder.T, preferred_element_type=jnp.float32),
            "lat",
            scatter_dimension=0,
            tiled=True,
        )
        grad_lower = grad_upper + owned_sum
        grads_new = lax.dynamic_update_index_in_dim(grads_acc, grad_lower, batch_index, 0)
        attrib_new = lax.dynamic_update_index_in_dim(attrib_acc, attrib_now, batch_index, 0)
        grads_acc = jnp.where(is_valid, grads_new, grads_acc)
        attrib_acc = jnp.where(is_valid, attrib_new, attrib_acc)
        return (grad_lower, full_upper, grads_acc, attrib_acc)

    final_state = lax.fori_loop(
        0,
        batch_count + section_count - 1,
        advance,
        (lower_init, above_init, grads_init, attrib_init),
    )
    return (final_state[2][None], final_state[3][None])


def solution(mesh):
    placed = (
        P("section", None, None, "lat"),
        P("section", None, "lat"),
        P("section", None, "lat"),
        P("section", "lat", None),
        P("section", "lat", None),
        P(None, "lat", None),
    )
    return jax.shard_map(
        local,
        mesh=mesh,
        in_specs=placed,
        out_specs=(P("section", None, "lat", None), P("section", None, None, "lat")),
        check_vma=False,
    )
```

profile of v0, /device:TPU:0, one launch (start us, length us, event | category | flops | bytes accessed | tf_op | source)
XLA Modules:
  0.0 485.7 jit_solution(16177794174378767081)
XLA Ops:
  7.3 471.0 %while.22 = (s32[]{:T(128)}, f32[16,2304]{1,0:T(8,128)S(1)}, bf16[64,2304]{1,0:T(8,128)(2,1)S(1)}, f32[2,16,2304]{2,1,0:T(8,128)S(1)}, bf16[2,64,2048]{2,1,0:T(8...) while((s32[]{:T(128)}, f32[16,2304]{1,0:T(8,128)S(1)}, ...), condition=%wide.region_2.3_spmd.clone, body=%wide.region_0.2_spmd.clone.sunk | while | flops 1813172224 | bytes 117588632 | solution.py:62
  7.4 1.4 collective-permute-start.1
  11.1 6.0 %collective-permute-done.1 = f32[16,2304]{1,0:T(8,128)S(1)} collective-permute-done((f32[16,2304]{1,0:T(8,128)S(1)}, f32[16,2304]{1,0:T(8,128)S(1)}, u32[]{:S(2)}, u32[]{:S(2)}) %collective-permute-start.1) | collective-permute-done | bytes 147488 | tf_op jit(solution)/shard_map/while/body/eval_jaxpr/ppermute | solution.py:10
  18.0 6.5 %all_gather.11 = bf16[64,2304]{1,0:T(8,128)(2,1)S(1)} all-gather(bf16[16,2304]{1,0:T(8,128)(2,1)S(1)} %fusion.37), channel_id=1, replica_groups=mesh['section'=8,'lat'=4] {'lat'}, dimensions={0}, use_global_device_ids=true | all-gather | bytes 368640 | tf_op jit(solution)/shard_map/while/body/eval_jaxpr/all_gather | solution.py:40
  24.5 6.8 %fusion.36 = f32[64,2048]{1,0:T(8,128)S(1)} fusion(bf16[64,2304]{1,0:T(8,128)(2,1)S(1)} %collective-permute-done, bf16[2048,2304]{1,0:T(8,128)(2,1)} %get-tuple-element.485), kind=kOutput, calls=%fused_computation.20.clone.1 | convolution fusion | flops 603979776 | bytes 10256384 | tf_op jit(solution)/shard_map/while/body/eval_jaxpr/dot_general | solution.py:42
  31.3 3.0 fusion.38
  34.3 3.8 fusion.39
  38.1 23.1 %reduce-scatter.2.cloned.1.call-done = f32[16,2304]{1,0:T(8,128)} async-done(((f32[64,2304]{1,0:T(8,128)}), f32[16,2304]{1,0:T(8,128)}) %reduce-scatter.2.cloned.1.call-update) | async-done | bytes 147472 | tf_op jit(solution)/shard_map/while/body/eval_jaxpr/reduce_scatter | solution.py:49
  62.2 1.4 collective-permute-start.1
  65.9 4.9 %collective-permute-done.1 = f32[16,2304]{1,0:T(8,128)S(1)} collective-permute-done((f32[16,2304]{1,0:T(8,128)S(1)}, f32[16,2304]{1,0:T(8,128)S(1)}, u32[]{:S(2)}, u32[]{:S(2)}) %collective-permute-start.1) | collective-permute-done | bytes 147488 | tf_op jit(solution)/shard_map/while/body/eval_jaxpr/ppermute | solution.py:10
  71.8 5.9 %all_gather.11 = bf16[64,2304]{1,0:T(8,128)(2,1)S(1)} all-gather(bf16[16,2304]{1,0:T(8,128)(2,1)S(1)} %fusion.37), channel_id=1, replica_groups=mesh['section'=8,'lat'=4] {'lat'}, dimensions={0}, use_global_device_ids=true | all-gather | bytes 368640 | tf_op jit(solution)/shard_map/while/body/eval_jaxpr/all_gather | solution.py:40
  77.7 6.8 %fusion.36 = f32[64,2048]{1,0:T(8,128)S(1)} fusion(bf16[64,2304]{1,0:T(8,128)(2,1)S(1)} %collective-permute-done, bf16[2048,2304]{1,0:T(8,128)(2,1)} %get-tuple-element.485), kind=kOutput, calls=%fused_computation.20.clone.1 | convolution fusion | flops 603979776 | bytes 10256384 | tf_op jit(solution)/shard_map/while/body/eval_jaxpr/dot_general | solution.py:42
  84.5 3.0 fusion.38
  87.4 3.8 fusion.39
  91.2 21.9 %reduce-scatter.2.cloned.1.call-done = f32[16,2304]{1,0:T(8,128)} async-done(((f32[64,2304]{1,0:T(8,128)}), f32[16,2304]{1,0:T(8,128)}) %reduce-scatter.2.cloned.1.call-update) | async-done | bytes 147472 | tf_op jit(solution)/shard_map/while/body/eval_jaxpr/reduce_scatter | solution.py:49
  114.2 1.4 collective-permute-start.1
  117.9 5.0 %collective-permute-done.1 = f32[16,2304]{1,0:T(8,128)S(1)} collective-permute-done((f32[16,2304]{1,0:T(8,128)S(1)}, f32[16,2304]{1,0:T(8,128)S(1)}, u32[]{:S(2)}, u32[]{:S(2)}) %collective-permute-start.1) | collective-permute-done | bytes 147488 | tf_op jit(solution)/shard_map/while/body/eval_jaxpr/ppermute | solution.py:10
  123.8 5.9 %all_gather.11 = bf16[64,2304]{1,0:T(8,128)(2,1)S(1)} all-gather(bf16[16,2304]{1,0:T(8,128)(2,1)S(1)} %fusion.37), channel_id=1, replica_groups=mesh['section'=8,'lat'=4] {'lat'}, dimensions={0}, use_global_device_ids=true | all-gather | bytes 368640 | tf_op jit(solution)/shard_map/while/body/eval_jaxpr/all_gather | solution.py:40
  129.7 6.8 %fusion.36 = f32[64,2048]{1,0:T(8,128)S(1)} fusion(bf16[64,2304]{1,0:T(8,128)(2,1)S(1)} %collective-permute-done, bf16[2048,2304]{1,0:T(8,128)(2,1)} %get-tuple-element.485), kind=kOutput, calls=%fused_computation.20.clone.1 | convolution fusion | flops 603979776 | bytes 10256384 | tf_op jit(solution)/shard_map/while/body/eval_jaxpr/dot_general | solution.py:42
  136.4 3.0 fusion.38
  139.4 3.8 fusion.39
  143.2 22.0 %reduce-scatter.2.cloned.1.call-done = f32[16,2304]{1,0:T(8,128)} async-done(((f32[64,2304]{1,0:T(8,128)}), f32[16,2304]{1,0:T(8,128)}) %reduce-scatter.2.cloned.1.call-update) | async-done | bytes 147472 | tf_op jit(solution)/shard_map/while/body/eval_jaxpr/reduce_scatter | solution.py:49
  166.2 1.4 collective-permute-start.1
  169.9 5.0 %collective-permute-done.1 = f32[16,2304]{1,0:T(8,128)S(1)} collective-permute-done((f32[16,2304]{1,0:T(8,128)S(1)}, f32[16,2304]{1,0:T(8,128)S(1)}, u32[]{:S(2)}, u32[]{:S(2)}) %collective-permute-start.1) | collective-permute-done | bytes 147488 | tf_op jit(solution)/shard_map/while/body/eval_jaxpr/ppermute | solution.py:10
  175.8 5.9 %all_gather.11 = bf16[64,2304]{1,0:T(8,128)(2,1)S(1)} all-gather(bf16[16,2304]{1,0:T(8,128)(2,1)S(1)} %fusion.37), channel_id=1, replica_groups=mesh['section'=8,'lat'=4] {'lat'}, dimensions={0}, use_global_device_ids=true | all-gather | bytes 368640 | tf_op jit(solution)/shard_map/while/body/eval_jaxpr/all_gather | solution.py:40
  181.7 6.8 %fusion.36 = f32[64,2048]{1,0:T(8,128)S(1)} fusion(bf16[64,2304]{1,0:T(8,128)(2,1)S(1)} %collective-permute-done, bf16[2048,2304]{1,0:T(8,128)(2,1)} %get-tuple-element.485), kind=kOutput, calls=%fused_computation.20.clone.1 | convolution fusion | flops 603979776 | bytes 10256384 | tf_op jit(solution)/shard_map/while/body/eval_jaxpr/dot_general | solution.py:42
  188.5 3.0 fusion.38
  191.5 3.8 fusion.39
  195.3 21.9 %reduce-scatter.2.cloned.1.call-done = f32[16,2304]{1,0:T(8,128)} async-done(((f32[64,2304]{1,0:T(8,128)}), f32[16,2304]{1,0:T(8,128)}) %reduce-scatter.2.cloned.1.call-update) | async-done | bytes 147472 | tf_op jit(solution)/shard_map/while/body/eval_jaxpr/reduce_scatter | solution.py:49
  218.3 1.4 collective-permute-start.1
  222.0 5.0 %collective-permute-done.1 = f32[16,2304]{1,0:T(8,128)S(1)} collective-permute-done((f32[16,2304]{1,0:T(8,128)S(1)}, f32[16,2304]{1,0:T(8,128)S(1)}, u32[]{:S(2)}, u32[]{:S(2)}) %collective-permute-start.1) | collective-permute-done | bytes 147488 | tf_op jit(solution)/shard_map/while/body/eval_jaxpr/ppermute | solution.py:10
  227.8 5.9 %all_gather.11 = bf16[64,2304]{1,0:T(8,128)(2,1)S(1)} all-gather(bf16[16,2304]{1,0:T(8,128)(2,1)S(1)} %fusion.37), channel_id=1, replica_groups=mesh['section'=8,'lat'=4] {'lat'}, dimensions={0}, use_global_device_ids=true | all-gather | bytes 368640 | tf_op jit(solution)/shard_map/while/body/eval_jaxpr/all_gather | solution.py:40
  233.7 6.8 %fusion.36 = f32[64,2048]{1,0:T(8,128)S(1)} fusion(bf16[64,2304]{1,0:T(8,128)(2,1)S(1)} %collective-permute-done, bf16[2048,2304]{1,0:T(8,128)(2,1)} %get-tuple-element.485), kind=kOutput, calls=%fused_computation.20.clone.1 | convolution fusion | flops 603979776 | bytes 10256384 | tf_op jit(solution)/shard_map/while/body/eval_jaxpr/dot_general | solution.py:42
  240.5 3.0 fusion.38
  243.5 3.8 fusion.39
  247.3 22.0 %reduce-scatter.2.cloned.1.call-done = f32[16,2304]{1,0:T(8,128)} async-done(((f32[64,2304]{1,0:T(8,128)}), f32[16,2304]{1,0:T(8,128)}) %reduce-scatter.2.cloned.1.call-update) | async-done | bytes 147472 | tf_op jit(solution)/shard_map/while/body/eval_jaxpr/reduce_scatter | solution.py:49
  270.3 1.4 collective-permute-start.1
  274.0 5.0 %collective-permute-done.1 = f32[16,2304]{1,0:T(8,128)S(1)} collective-permute-done((f32[16,2304]{1,0:T(8,128)S(1)}, f32[16,2304]{1,0:T(8,128)S(1)}, u32[]{:S(2)}, u32[]{:S(2)}) %collective-permute-start.1) | collective-permute-done | bytes 147488 | tf_op jit(solution)/shard_map/while/body/eval_jaxpr/ppermute | solution.py:10
  279.9 5.9 %all_gather.11 = bf16[64,2304]{1,0:T(8,128)(2,1)S(1)} all-gather(bf16[16,2304]{1,0:T(8,128)(2,1)S(1)} %fusion.37), channel_id=1, replica_groups=mesh['section'=8,'lat'=4] {'lat'}, dimensions={0}, use_global_device_ids=true | all-gather | bytes 368640 | tf_op jit(solution)/shard_map/while/body/eval_jaxpr/all_gather | solution.py:40
  285.8 6.8 %fusion.36 = f32[64,2048]{1,0:T(8,128)S(1)} fusion(bf16[64,2304]{1,0:T(8,128)(2,1)S(1)} %collective-permute-done, bf16[2048,2304]{1,0:T(8,128)(2,1)} %get-tuple-element.485), kind=kOutput, calls=%fused_computation.20.clone.1 | convolution fusion | flops 603979776 | bytes 10256384 | tf_op jit(solution)/shard_map/while/body/eval_jaxpr/dot_general | solution.py:42
  292.6 3.0 fusion.38
  295.5 3.8 fusion.39
  299.3 21.9 %reduce-scatter.2.cloned.1.call-done = f32[16,2304]{1,0:T(8,128)} async-done(((f32[64,2304]{1,0:T(8,128)}), f32[16,2304]{1,0:T(8,128)}) %reduce-scatter.2.cloned.1.call-update) | async-done | bytes 147472 | tf_op jit(solution)/shard_map/while/body/eval_jaxpr/reduce_scatter | solution.py:49
  322.3 1.4 collective-permute-start.1
  326.0 5.0 %collective-permute-done.1 = f32[16,2304]{1,0:T(8,128)S(1)} collective-permute-done((f32[16,2304]{1,0:T(8,128)S(1)}, f32[16,2304]{1,0:T(8,128)S(1)}, u32[]{:S(2)}, u32[]{:S(2)}) %collective-permute-start.1) | collective-permute-done | bytes 147488 | tf_op jit(solution)/shard_map/while/body/eval_jaxpr/ppermute | solution.py:10
  331.9 5.9 %all_gather.11 = bf16[64,2304]{1,0:T(8,128)(2,1)S(1)} all-gather(bf16[16,2304]{1,0:T(8,128)(2,1)S(1)} %fusion.37), channel_id=1, replica_groups=mesh['section'=8,'lat'=4] {'lat'}, dimensions={0}, use_global_device_ids=true | all-gather | bytes 368640 | tf_op jit(solution)/shard_map/while/body/eval_jaxpr/all_gather | solution.py:40
  337.7 6.8 %fusion.36 = f32[64,2048]{1,0:T(8,128)S(1)} fusion(bf16[64,2304]{1,0:T(8,128)(2,1)S(1)} %collective-permute-done, bf16[2048,2304]{1,0:T(8,128)(2,1)} %get-tuple-element.485), kind=kOutput, calls=%fused_computation.20.clone.1 | convolution fusion | flops 603979776 | bytes 10256384 | tf_op jit(solution)/shard_map/while/body/eval_jaxpr/dot_general | solution.py:42
  344.5 3.0 fusion.38
  347.5 3.8 fusion.39
  351.3 21.9 %reduce-scatter.2.cloned.1.call-done = f32[16,2304]{1,0:T(8,128)} async-done(((f32[64,2304]{1,0:T(8,128)}), f32[16,2304]{1,0:T(8,128)}) %reduce-scatter.2.cloned.1.call-update) | async-done | bytes 147472 | tf_op jit(solution)/shard_map/while/body/eval_jaxpr/reduce_scatter | solution.py:49
  374.3 1.4 collective-permute-start.1
  378.0 5.0 %collective-permute-done.1 = f32[16,2304]{1,0:T(8,128)S(1)} collective-permute-done((f32[16,2304]{1,0:T(8,128)S(1)}, f32[16,2304]{1,0:T(8,128)S(1)}, u32[]{:S(2)}, u32[]{:S(2)}) %collective-permute-start.1) | collective-permute-done | bytes 147488 | tf_op jit(solution)/shard_map/while/body/eval_jaxpr/ppermute | solution.py:10
  383.9 5.9 %all_gather.11 = bf16[64,2304]{1,0:T(8,128)(2,1)S(1)} all-gather(bf16[16,2304]{1,0:T(8,128)(2,1)S(1)} %fusion.37), channel_id=1, replica_groups=mesh['section'=8,'lat'=4] {'lat'}, dimensions={0}, use_global_device_ids=true | all-gather | bytes 368640 | tf_op jit(solution)/shard_map/while/body/eval_jaxpr/all_gather | solution.py:40
  389.8 6.8 %fusion.36 = f32[64,2048]{1,0:T(8,128)S(1)} fusion(bf16[64,2304]{1,0:T(8,128)(2,1)S(1)} %collective-permute-done, bf16[2048,2304]{1,0:T(8,128)(2,1)} %get-tuple-element.485), kind=kOutput, calls=%fused_computation.20.clone.1 | convolution fusion | flops 603979776 | bytes 10256384 | tf_op jit(solution)/shard_map/while/body/eval_jaxpr/dot_general | solution.py:42
  396.6 3.0 fusion.38
  399.5 3.8 fusion.39
  403.3 21.9 %reduce-scatter.2.cloned.1.call-done = f32[16,2304]{1,0:T(8,128)} async-done(((f32[64,2304]{1,0:T(8,128)}), f32[16,2304]{1,0:T(8,128)}) %reduce-scatter.2.cloned.1.call-update) | async-done | bytes 147472 | tf_op jit(solution)/shard_map/while/body/eval_jaxpr/reduce_scatter | solution.py:49
  426.3 1.4 collective-permute-start.1
  430.0 5.0 %collective-permute-done.1 = f32[16,2304]{1,0:T(8,128)S(1)} collective-permute-done((f32[16,2304]{1,0:T(8,128)S(1)}, f32[16,2304]{1,0:T(8,128)S(1)}, u32[]{:S(2)}, u32[]{:S(2)}) %collective-permute-start.1) | collective-permute-done | bytes 147488 | tf_op jit(solution)/shard_map/while/body/eval_jaxpr/ppermute | solution.py:10
  435.9 5.9 %all_gather.11 = bf16[64,2304]{1,0:T(8,128)(2,1)S(1)} all-gather(bf16[16,2304]{1,0:T(8,128)(2,1)S(1)} %fusion.37), channel_id=1, replica_groups=mesh['section'=8,'lat'=4] {'lat'}, dimensions={0}, use_global_device_ids=true | all-gather | bytes 368640 | tf_op jit(solution)/shard_map/while/body/eval_jaxpr/all_gather | solution.py:40
  441.8 6.8 %fusion.36 = f32[64,2048]{1,0:T(8,128)S(1)} fusion(bf16[64,2304]{1,0:T(8,128)(2,1)S(1)} %collective-permute-done, bf16[2048,2304]{1,0:T(8,128)(2,1)} %get-tuple-element.485), kind=kOutput, calls=%fused_computation.20.clone.1 | convolution fusion | flops 603979776 | bytes 10256384 | tf_op jit(solution)/shard_map/while/body/eval_jaxpr/dot_general | solution.py:42
  448.6 3.0 fusion.38
  451.6 3.8 fusion.39
  455.4 22.0 %reduce-scatter.2.cloned.1.call-done = f32[16,2304]{1,0:T(8,128)} async-done(((f32[64,2304]{1,0:T(8,128)}), f32[16,2304]{1,0:T(8,128)}) %reduce-scatter.2.cloned.1.call-update) | async-done | bytes 147472 | tf_op jit(solution)/shard_map/while/body/eval_jaxpr/reduce_scatter | solution.py:49
  (170 shorter events, 38.7 us)
Async XLA Ops:
  7.3 24.0 %copy-start.5 = (bf16[1,2,64,2048]{3,2,1,0:T(8,128)(2,1)S(1)}, bf16[1,2,64,2048]{3,2,1,0:T(8,128)(2,1)}, u32[]{:S(2)}) copy-start(bf16[1,2,64,2048]{3,2,1,0:T(8,128)(2,1)} %get-tuple-element.488) | copy-start | bytes 1572868 | tf_op jit(solution)/shard_map/while
  7.3 53.9 %reduce-scatter.2.cloned.1.call-start = ((), (), s32[]{:S(2)}) async-start(), calls=%async_computation.1 | async-start | bytes 737280 | tf_op jit(solution)/shard_map/while/body/eval_jaxpr/reduce_scatter | solution.py:49
  7.4 9.7 %collective-permute-start.1 = (f32[16,2304]{1,0:T(8,128)S(1)}, f32[16,2304]{1,0:T(8,128)S(1)}, u32[]{:S(2)}, u32[]{:S(2)}) collective-permute-start(f32[16,2304]{1,0:T(8,128)S(1)} %broadcast_select_fusion.2), channel_id=1, source_target_pairs={{4,0},{8,4},{12,8},{16,12},{20,16},{24,20},{28,24},{5,1},{9,5},{13... | collective-permute-start | bytes 442376 | tf_op jit(solution)/shard_map/while/body/eval_jaxpr/ppermute | solution.py:10
  8.9 15.6 %collective-permute-start = (bf16[64,2304]{1,0:T(8,128)(2,1)S(1)}, bf16[64,2304]{1,0:T(8,128)(2,1)S(1)}, u32[]{:S(2)}, u32[]{:S(2)}) collective-permute-start(bf16[64,2304]{1,0:T(8,128)(2,1)S(1)} %copy.17), channel_id=1, source_target_pairs={{4,0},{8,4},{12,8},{16,12},{20,16},{24,20},{28,24},{5,1},{9,5},{13... | collective-permute-start | bytes 884744 | tf_op jit(solution)/shard_map/while/body/eval_jaxpr/ppermute | solution.py:10
  10.2 21.1 %copy-start = (bf16[2048,2304]{1,0:T(8,128)(2,1)S(1)}, bf16[2048,2304]{1,0:T(8,128)(2,1)}, u32[]{:S(2)}) copy-start(bf16[2048,2304]{1,0:T(8,128)(2,1)} %get-tuple-element.484) | copy-start | bytes 28311556 | tf_op jit(solution)/shard_map/while
  24.5 9.8 %copy-start.1 = (bf16[2304,2048]{1,0:T(8,128)(2,1)S(1)}, bf16[2304,2048]{1,0:T(8,128)(2,1)}, u32[]{:S(2)}) copy-start(bf16[2304,2048]{1,0:T(8,128)(2,1)} %get-tuple-element.487) | copy-start | bytes 28311556 | tf_op jit(solution)/shard_map/while
  31.3 29.9 %copy-start.3 = (f32[2,16,2304]{2,1,0:T(8,128)S(1)}, f32[2,16,2304]{2,1,0:T(8,128)}, u32[]{:S(2)}) copy-start(f32[2,16,2304]{2,1,0:T(8,128)} %get-tuple-element.483) | copy-start | bytes 884740 | tf_op jit(solution)/shard_map/while
  62.1 22.3 %copy-start.5 = (bf16[1,2,64,2048]{3,2,1,0:T(8,128)(2,1)S(1)}, bf16[1,2,64,2048]{3,2,1,0:T(8,128)(2,1)}, u32[]{:S(2)}) copy-start(bf16[1,2,64,2048]{3,2,1,0:T(8,128)(2,1)} %get-tuple-element.488) | copy-start | bytes 1572868 | tf_op jit(solution)/shard_map/while
  62.2 51.0 %reduce-scatter.2.cloned.1.call-start = ((), (), s32[]{:S(2)}) async-start(), calls=%async_computation.1 | async-start | bytes 737280 | tf_op jit(solution)/shard_map/while/body/eval_jaxpr/reduce_scatter | solution.py:49
  62.2 8.6 %collective-permute-start.1 = (f32[16,2304]{1,0:T(8,128)S(1)}, f32[16,2304]{1,0:T(8,128)S(1)}, u32[]{:S(2)}, u32[]{:S(2)}) collective-permute-start(f32[16,2304]{1,0:T(8,128)S(1)} %broadcast_select_fusion.2), channel_id=1, source_target_pairs={{4,0},{8,4},{12,8},{16,12},{20,16},{24,20},{28,24},{5,1},{9,5},{13... | collective-permute-start | bytes 442376 | tf_op jit(solution)/shard_map/while/body/eval_jaxpr/ppermute | solution.py:10
  63.7 14.0 %collective-permute-start = (bf16[64,2304]{1,0:T(8,128)(2,1)S(1)}, bf16[64,2304]{1,0:T(8,128)(2,1)S(1)}, u32[]{:S(2)}, u32[]{:S(2)}) collective-permute-start(bf16[64,2304]{1,0:T(8,128)(2,1)S(1)} %copy.17), channel_id=1, source_target_pairs={{4,0},{8,4},{12,8},{16,12},{20,16},{24,20},{28,24},{5,1},{9,5},{13... | collective-permute-start | bytes 884744 | tf_op jit(solution)/shard_map/while/body/eval_jaxpr/ppermute | solution.py:10
  65.0 19.4 %copy-start = (bf16[2048,2304]{1,0:T(8,128)(2,1)S(1)}, bf16[2048,2304]{1,0:T(8,128)(2,1)}, u32[]{:S(2)}) copy-start(bf16[2048,2304]{1,0:T(8,128)(2,1)} %get-tuple-element.484) | copy-start | bytes 28311556 | tf_op jit(solution)/shard_map/while
  77.7 9.8 %copy-start.1 = (bf16[2304,2048]{1,0:T(8,128)(2,1)S(1)}, bf16[2304,2048]{1,0:T(8,128)(2,1)}, u32[]{:S(2)}) copy-start(bf16[2304,2048]{1,0:T(8,128)(2,1)} %get-tuple-element.487) | copy-start | bytes 28311556 | tf_op jit(solution)/shard_map/while
  84.4 28.7 %copy-start.3 = (f32[2,16,2304]{2,1,0:T(8,128)S(1)}, f32[2,16,2304]{2,1,0:T(8,128)}, u32[]{:S(2)}) copy-start(f32[2,16,2304]{2,1,0:T(8,128)} %get-tuple-element.483) | copy-start | bytes 884740 | tf_op jit(solution)/shard_map/while
  114.1 22.3 %copy-start.5 = (bf16[1,2,64,2048]{3,2,1,0:T(8,128)(2,1)S(1)}, bf16[1,2,64,2048]{3,2,1,0:T(8,128)(2,1)}, u32[]{:S(2)}) copy-start(bf16[1,2,64,2048]{3,2,1,0:T(8,128)(2,1)} %get-tuple-element.488) | copy-start | bytes 1572868 | tf_op jit(solution)/shard_map/while
  114.1 51.1 %reduce-scatter.2.cloned.1.call-start = ((), (), s32[]{:S(2)}) async-start(), calls=%async_computation.1 | async-start | bytes 737280 | tf_op jit(solution)/shard_map/while/body/eval_jaxpr/reduce_scatter | solution.py:49
  114.2 8.6 %collective-permute-start.1 = (f32[16,2304]{1,0:T(8,128)S(1)}, f32[16,2304]{1,0:T(8,128)S(1)}, u32[]{:S(2)}, u32[]{:S(2)}) collective-permute-start(f32[16,2304]{1,0:T(8,128)S(1)} %broadcast_select_fusion.2), channel_id=1, source_target_pairs={{4,0},{8,4},{12,8},{16,12},{20,16},{24,20},{28,24},{5,1},{9,5},{13... | collective-permute-start | bytes 442376 | tf_op jit(solution)/shard_map/while/body/eval_jaxpr/ppermute | solution.py:10
  115.7 14.0 %collective-permute-start = (bf16[64,2304]{1,0:T(8,128)(2,1)S(1)}, bf16[64,2304]{1,0:T(8,128)(2,1)S(1)}, u32[]{:S(2)}, u32[]{:S(2)}) collective-permute-start(bf16[64,2304]{1,0:T(8,128)(2,1)S(1)} %copy.17), channel_id=1, source_target_pairs={{4,0},{8,4},{12,8},{16,12},{20,16},{24,20},{28,24},{5,1},{9,5},{13... | collective-permute-start | bytes 884744 | tf_op jit(solution)/shard_map/while/body/eval_jaxpr/ppermute | solution.py:10
  117.0 19.5 %copy-start = (bf16[2048,2304]{1,0:T(8,128)(2,1)S(1)}, bf16[2048,2304]{1,0:T(8,128)(2,1)}, u32[]{:S(2)}) copy-start(bf16[2048,2304]{1,0:T(8,128)(2,1)} %get-tuple-element.484) | copy-start | bytes 28311556 | tf_op jit(solution)/shard_map/while
  129.7 9.8 %copy-start.1 = (bf16[2304,2048]{1,0:T(8,128)(2,1)S(1)}, bf16[2304,2048]{1,0:T(8,128)(2,1)}, u32[]{:S(2)}) copy-start(bf16[2304,2048]{1,0:T(8,128)(2,1)} %get-tuple-element.487) | copy-start | bytes 28311556 | tf_op jit(solution)/shard_map/while
  136.4 28.7 %copy-start.3 = (f32[2,16,2304]{2,1,0:T(8,128)S(1)}, f32[2,16,2304]{2,1,0:T(8,128)}, u32[]{:S(2)}) copy-start(f32[2,16,2304]{2,1,0:T(8,128)} %get-tuple-element.483) | copy-start | bytes 884740 | tf_op jit(solution)/shard_map/while
  166.2 22.3 %copy-start.5 = (bf16[1,2,64,2048]{3,2,1,0:T(8,128)(2,1)S(1)}, bf16[1,2,64,2048]{3,2,1,0:T(8,128)(2,1)}, u32[]{:S(2)}) copy-start(bf16[1,2,64,2048]{3,2,1,0:T(8,128)(2,1)} %get-tuple-element.488) | copy-start | bytes 1572868 | tf_op jit(solution)/shard_map/while
  166.2 51.0 %reduce-scatter.2.cloned.1.call-start = ((), (), s32[]{:S(2)}) async-start(), calls=%async_computation.1 | async-start | bytes 737280 | tf_op jit(solution)/shard_map/while/body/eval_jaxpr/reduce_scatter | solution.py:49
  166.2 8.7 %collective-permute-start.1 = (f32[16,2304]{1,0:T(8,128)S(1)}, f32[16,2304]{1,0:T(8,128)S(1)}, u32[]{:S(2)}, u32[]{:S(2)}) collective-permute-start(f32[16,2304]{1,0:T(8,128)S(1)} %broadcast_select_fusion.2), channel_id=1, source_target_pairs={{4,0},{8,4},{12,8},{16,12},{20,16},{24,20},{28,24},{5,1},{9,5},{13... | collective-permute-start | bytes 442376 | tf_op jit(solution)/shard_map/while/body/eval_jaxpr/ppermute | solution.py:10
  167.7 14.0 %collective-permute-start = (bf16[64,2304]{1,0:T(8,128)(2,1)S(1)}, bf16[64,2304]{1,0:T(8,128)(2,1)S(1)}, u32[]{:S(2)}, u32[]{:S(2)}) collective-permute-start(bf16[64,2304]{1,0:T(8,128)(2,1)S(1)} %copy.17), channel_id=1, source_target_pairs={{4,0},{8,4},{12,8},{16,12},{20,16},{24,20},{28,24},{5,1},{9,5},{13... | collective-permute-start | bytes 884744 | tf_op jit(solution)/shard_map/while/body/eval_jaxpr/ppermute | solution.py:10
  169.0 19.5 %copy-start = (bf16[2048,2304]{1,0:T(8,128)(2,1)S(1)}, bf16[2048,2304]{1,0:T(8,128)(2,1)}, u32[]{:S(2)}) copy-start(bf16[2048,2304]{1,0:T(8,128)(2,1)} %get-tuple-element.484) | copy-start | bytes 28311556 | tf_op jit(solution)/shard_map/while
  181.7 9.8 %copy-start.1 = (bf16[2304,2048]{1,0:T(8,128)(2,1)S(1)}, bf16[2304,2048]{1,0:T(8,128)(2,1)}, u32[]{:S(2)}) copy-start(bf16[2304,2048]{1,0:T(8,128)(2,1)} %get-tuple-element.487) | copy-start | bytes 28311556 | tf_op jit(solution)/shard_map/while
  188.5 28.7 %copy-start.3 = (f32[2,16,2304]{2,1,0:T(8,128)S(1)}, f32[2,16,2304]{2,1,0:T(8,128)}, u32[]{:S(2)}) copy-start(f32[2,16,2304]{2,1,0:T(8,128)} %get-tuple-element.483) | copy-start | bytes 884740 | tf_op jit(solution)/shard_map/while
  218.2 22.3 %copy-start.5 = (bf16[1,2,64,2048]{3,2,1,0:T(8,128)(2,1)S(1)}, bf16[1,2,64,2048]{3,2,1,0:T(8,128)(2,1)}, u32[]{:S(2)}) copy-start(bf16[1,2,64,2048]{3,2,1,0:T(8,128)(2,1)} %get-tuple-element.488) | copy-start | bytes 1572868 | tf_op jit(solution)/shard_map/while
  218.2 51.1 %reduce-scatter.2.cloned.1.call-start = ((), (), s32[]{:S(2)}) async-start(), calls=%async_computation.1 | async-start | bytes 737280 | tf_op jit(solution)/shard_map/while/body/eval_jaxpr/reduce_scatter | solution.py:49
  218.3 8.6 %collective-permute-start.1 = (f32[16,2304]{1,0:T(8,128)S(1)}, f32[16,2304]{1,0:T(8,128)S(1)}, u32[]{:S(2)}, u32[]{:S(2)}) collective-permute-start(f32[16,2304]{1,0:T(8,128)S(1)} %broadcast_select_fusion.2), channel_id=1, source_target_pairs={{4,0},{8,4},{12,8},{16,12},{20,16},{24,20},{28,24},{5,1},{9,5},{13... | collective-permute-start | bytes 442376 | tf_op jit(solution)/shard_map/while/body/eval_jaxpr/ppermute | solution.py:10
  219.7 14.0 %collective-permute-start = (bf16[64,2304]{1,0:T(8,128)(2,1)S(1)}, bf16[64,2304]{1,0:T(8,128)(2,1)S(1)}, u32[]{:S(2)}, u32[]{:S(2)}) collective-permute-start(bf16[64,2304]{1,0:T(8,128)(2,1)S(1)} %copy.17), channel_id=1, source_target_pairs={{4,0},{8,4},{12,8},{16,12},{20,16},{24,20},{28,24},{5,1},{9,5},{13... | collective-permute-start | bytes 884744 | tf_op jit(solution)/shard_map/while/body/eval_jaxpr/ppermute | solution.py:10
  221.0 19.5 %copy-start = (bf16[2048,2304]{1,0:T(8,128)(2,1)S(1)}, bf16[2048,2304]{1,0:T(8,128)(2,1)}, u32[]{:S(2)}) copy-start(bf16[2048,2304]{1,0:T(8,128)(2,1)} %get-tuple-element.484) | copy-start | bytes 28311556 | tf_op jit(solution)/shard_map/while
  233.7 9.8 %copy-start.1 = (bf16[2304,2048]{1,0:T(8,128)(2,1)S(1)}, bf16[2304,2048]{1,0:T(8,128)(2,1)}, u32[]{:S(2)}) copy-start(bf16[2304,2048]{1,0:T(8,128)(2,1)} %get-tuple-element.487) | copy-start | bytes 28311556 | tf_op jit(solution)/shard_map/while
  240.5 28.8 %copy-start.3 = (f32[2,16,2304]{2,1,0:T(8,128)S(1)}, f32[2,16,2304]{2,1,0:T(8,128)}, u32[]{:S(2)}) copy-start(f32[2,16,2304]{2,1,0:T(8,128)} %get-tuple-element.483) | copy-start | bytes 884740 | tf_op jit(solution)/shard_map/while
  270.2 22.3 %copy-start.5 = (bf16[1,2,64,2048]{3,2,1,0:T(8,128)(2,1)S(1)}, bf16[1,2,64,2048]{3,2,1,0:T(8,128)(2,1)}, u32[]{:S(2)}) copy-start(bf16[1,2,64,2048]{3,2,1,0:T(8,128)(2,1)} %get-tuple-element.488) | copy-start | bytes 1572868 | tf_op jit(solution)/shard_map/while
  270.2 51.0 %reduce-scatter.2.cloned.1.call-start = ((), (), s32[]{:S(2)}) async-start(), calls=%async_computation.1 | async-start | bytes 737280 | tf_op jit(solution)/shard_map/while/body/eval_jaxpr/reduce_scatter | solution.py:49
  270.3 8.7 %collective-permute-start.1 = (f32[16,2304]{1,0:T(8,128)S(1)}, f32[16,2304]{1,0:T(8,128)S(1)}, u32[]{:S(2)}, u32[]{:S(2)}) collective-permute-start(f32[16,2304]{1,0:T(8,128)S(1)} %broadcast_select_fusion.2), channel_id=1, source_target_pairs={{4,0},{8,4},{12,8},{16,12},{20,16},{24,20},{28,24},{5,1},{9,5},{13... | collective-permute-start | bytes 442376 | tf_op jit(solution)/shard_map/while/body/eval_jaxpr/ppermute | solution.py:10
  271.8 14.0 %collective-permute-start = (bf16[64,2304]{1,0:T(8,128)(2,1)S(1)}, bf16[64,2304]{1,0:T(8,128)(2,1)S(1)}, u32[]{:S(2)}, u32[]{:S(2)}) collective-permute-start(bf16[64,2304]{1,0:T(8,128)(2,1)S(1)} %copy.17), channel_id=1, source_target_pairs={{4,0},{8,4},{12,8},{16,12},{20,16},{24,20},{28,24},{5,1},{9,5},{13... | collective-permute-start | bytes 884744 | tf_op jit(solution)/shard_map/while/body/eval_jaxpr/ppermute | solution.py:10
  273.1 19.5 %copy-start = (bf16[2048,2304]{1,0:T(8,128)(2,1)S(1)}, bf16[2048,2304]{1,0:T(8,128)(2,1)}, u32[]{:S(2)}) copy-start(bf16[2048,2304]{1,0:T(8,128)(2,1)} %get-tuple-element.484) | copy-start | bytes 28311556 | tf_op jit(solution)/shard_map/while
  285.8 9.8 %copy-start.1 = (bf16[2304,2048]{1,0:T(8,128)(2,1)S(1)}, bf16[2304,2048]{1,0:T(8,128)(2,1)}, u32[]{:S(2)}) copy-start(bf16[2304,2048]{1,0:T(8,128)(2,1)} %get-tuple-element.487) | copy-start | bytes 28311556 | tf_op jit(solution)/shard_map/while
  292.5 28.7 %copy-start.3 = (f32[2,16,2304]{2,1,0:T(8,128)S(1)}, f32[2,16,2304]{2,1,0:T(8,128)}, u32[]{:S(2)}) copy-start(f32[2,16,2304]{2,1,0:T(8,128)} %get-tuple-element.483) | copy-start | bytes 884740 | tf_op jit(solution)/shard_map/while
  322.2 22.3 %copy-start.5 = (bf16[1,2,64,2048]{3,2,1,0:T(8,128)(2,1)S(1)}, bf16[1,2,64,2048]{3,2,1,0:T(8,128)(2,1)}, u32[]{:S(2)}) copy-start(bf16[1,2,64,2048]{3,2,1,0:T(8,128)(2,1)} %get-tuple-element.488) | copy-start | bytes 1572868 | tf_op jit(solution)/shard_map/while
  322.2 51.0 %reduce-scatter.2.cloned.1.call-start = ((), (), s32[]{:S(2)}) async-start(), calls=%async_computation.1 | async-start | bytes 737280 | tf_op jit(solution)/shard_map/while/body/eval_jaxpr/reduce_scatter | solution.py:49
  322.3 8.7 %collective-permute-start.1 = (f32[16,2304]{1,0:T(8,128)S(1)}, f32[16,2304]{1,0:T(8,128)S(1)}, u32[]{:S(2)}, u32[]{:S(2)}) collective-permute-start(f32[16,2304]{1,0:T(8,128)S(1)} %broadcast_select_fusion.2), channel_id=1, source_target_pairs={{4,0},{8,4},{12,8},{16,12},{20,16},{24,20},{28,24},{5,1},{9,5},{13... | collective-permute-start | bytes 442376 | tf_op jit(solution)/shard_map/while/body/eval_jaxpr/ppermute | solution.py:10
  323.7 14.0 %collective-permute-start = (bf16[64,2304]{1,0:T(8,128)(2,1)S(1)}, bf16[64,2304]{1,0:T(8,128)(2,1)S(1)}, u32[]{:S(2)}, u32[]{:S(2)}) collective-permute-start(bf16[64,2304]{1,0:T(8,128)(2,1)S(1)} %copy.17), channel_id=1, source_target_pairs={{4,0},{8,4},{12,8},{16,12},{20,16},{24,20},{28,24},{5,1},{9,5},{13... | collective-permute-start | bytes 884744 | tf_op jit(solution)/shard_map/while/body/eval_jaxpr/ppermute | solution.py:10
  325.1 19.5 %copy-start = (bf16[2048,2304]{1,0:T(8,128)(2,1)S(1)}, bf16[2048,2304]{1,0:T(8,128)(2,1)}, u32[]{:S(2)}) copy-start(bf16[2048,2304]{1,0:T(8,128)(2,1)} %get-tuple-element.484) | copy-start | bytes 28311556 | tf_op jit(solution)/shard_map/while
  337.7 9.8 %copy-start.1 = (bf16[2304,2048]{1,0:T(8,128)(2,1)S(1)}, bf16[2304,2048]{1,0:T(8,128)(2,1)}, u32[]{:S(2)}) copy-start(bf16[2304,2048]{1,0:T(8,128)(2,1)} %get-tuple-element.487) | copy-start | bytes 28311556 | tf_op jit(solution)/shard_map/while
  344.5 28.7 %copy-start.3 = (f32[2,16,2304]{2,1,0:T(8,128)S(1)}, f32[2,16,2304]{2,1,0:T(8,128)}, u32[]{:S(2)}) copy-start(f32[2,16,2304]{2,1,0:T(8,128)} %get-tuple-element.483) | copy-start | bytes 884740 | tf_op jit(solution)/shard_map/while
  374.2 22.3 %copy-start.5 = (bf16[1,2,64,2048]{3,2,1,0:T(8,128)(2,1)S(1)}, bf16[1,2,64,2048]{3,2,1,0:T(8,128)(2,1)}, u32[]{:S(2)}) copy-start(bf16[1,2,64,2048]{3,2,1,0:T(8,128)(2,1)} %get-tuple-element.488) | copy-start | bytes 1572868 | tf_op jit(solution)/shard_map/while
  374.2 51.0 %reduce-scatter.2.cloned.1.call-start = ((), (), s32[]{:S(2)}) async-start(), calls=%async_computation.1 | async-start | bytes 737280 | tf_op jit(solution)/shard_map/while/body/eval_jaxpr/reduce_scatter | solution.py:49
  374.3 8.7 %collective-permute-start.1 = (f32[16,2304]{1,0:T(8,128)S(1)}, f32[16,2304]{1,0:T(8,128)S(1)}, u32[]{:S(2)}, u32[]{:S(2)}) collective-permute-start(f32[16,2304]{1,0:T(8,128)S(1)} %broadcast_select_fusion.2), channel_id=1, source_target_pairs={{4,0},{8,4},{12,8},{16,12},{20,16},{24,20},{28,24},{5,1},{9,5},{13... | collective-permute-start | bytes 442376 | tf_op jit(solution)/shard_map/while/body/eval_jaxpr/ppermute | solution.py:10
  375.8 14.0 %collective-permute-start = (bf16[64,2304]{1,0:T(8,128)(2,1)S(1)}, bf16[64,2304]{1,0:T(8,128)(2,1)S(1)}, u32[]{:S(2)}, u32[]{:S(2)}) collective-permute-start(bf16[64,2304]{1,0:T(8,128)(2,1)S(1)} %copy.17), channel_id=1, source_target_pairs={{4,0},{8,4},{12,8},{16,12},{20,16},{24,20},{28,24},{5,1},{9,5},{13... | collective-permute-start | bytes 884744 | tf_op jit(solution)/shard_map/while/body/eval_jaxpr/ppermute | solution.py:10
  377.1 19.5 %copy-start = (bf16[2048,2304]{1,0:T(8,128)(2,1)S(1)}, bf16[2048,2304]{1,0:T(8,128)(2,1)}, u32[]{:S(2)}) copy-start(bf16[2048,2304]{1,0:T(8,128)(2,1)} %get-tuple-element.484) | copy-start | bytes 28311556 | tf_op jit(solution)/shard_map/while
  389.8 9.8 %copy-start.1 = (bf16[2304,2048]{1,0:T(8,128)(2,1)S(1)}, bf16[2304,2048]{1,0:T(8,128)(2,1)}, u32[]{:S(2)}) copy-start(bf16[2304,2048]{1,0:T(8,128)(2,1)} %get-tuple-element.487) | copy-start | bytes 28311556 | tf_op jit(solution)/shard_map/while
  396.5 28.7 %copy-start.3 = (f32[2,16,2304]{2,1,0:T(8,128)S(1)}, f32[2,16,2304]{2,1,0:T(8,128)}, u32[]{:S(2)}) copy-start(f32[2,16,2304]{2,1,0:T(8,128)} %get-tuple-element.483) | copy-start | bytes 884740 | tf_op jit(solution)/shard_map/while
  426.2 22.3 %copy-start.5 = (bf16[1,2,64,2048]{3,2,1,0:T(8,128)(2,1)S(1)}, bf16[1,2,64,2048]{3,2,1,0:T(8,128)(2,1)}, u32[]{:S(2)}) copy-start(bf16[1,2,64,2048]{3,2,1,0:T(8,128)(2,1)} %get-tuple-element.488) | copy-start | bytes 1572868 | tf_op jit(solution)/shard_map/while
  426.3 51.1 %reduce-scatter.2.cloned.1.call-start = ((), (), s32[]{:S(2)}) async-start(), calls=%async_computation.1 | async-start | bytes 737280 | tf_op jit(solution)/shard_map/while/body/eval_jaxpr/reduce_scatter | solution.py:49
  426.3 8.6 %collective-permute-start.1 = (f32[16,2304]{1,0:T(8,128)S(1)}, f32[16,2304]{1,0:T(8,128)S(1)}, u32[]{:S(2)}, u32[]{:S(2)}) collective-permute-start(f32[16,2304]{1,0:T(8,128)S(1)} %broadcast_select_fusion.2), channel_id=1, source_target_pairs={{4,0},{8,4},{12,8},{16,12},{20,16},{24,20},{28,24},{5,1},{9,5},{13... | collective-permute-start | bytes 442376 | tf_op jit(solution)/shard_map/while/body/eval_jaxpr/ppermute | solution.py:10
  427.8 14.0 %collective-permute-start = (bf16[64,2304]{1,0:T(8,128)(2,1)S(1)}, bf16[64,2304]{1,0:T(8,128)(2,1)S(1)}, u32[]{:S(2)}, u32[]{:S(2)}) collective-permute-start(bf16[64,2304]{1,0:T(8,128)(2,1)S(1)} %copy.17), channel_id=1, source_target_pairs={{4,0},{8,4},{12,8},{16,12},{20,16},{24,20},{28,24},{5,1},{9,5},{13... | collective-permute-start | bytes 884744 | tf_op jit(solution)/shard_map/while/body/eval_jaxpr/ppermute | solution.py:10
  429.1 19.5 %copy-start = (bf16[2048,2304]{1,0:T(8,128)(2,1)S(1)}, bf16[2048,2304]{1,0:T(8,128)(2,1)}, u32[]{:S(2)}) copy-start(bf16[2048,2304]{1,0:T(8,128)(2,1)} %get-tuple-element.484) | copy-start | bytes 28311556 | tf_op jit(solution)/shard_map/while
  441.8 9.8 %copy-start.1 = (bf16[2304,2048]{1,0:T(8,128)(2,1)S(1)}, bf16[2304,2048]{1,0:T(8,128)(2,1)}, u32[]{:S(2)}) copy-start(bf16[2304,2048]{1,0:T(8,128)(2,1)} %get-tuple-element.487) | copy-start | bytes 28311556 | tf_op jit(solution)/shard_map/while
  448.6 28.8 %copy-start.3 = (f32[2,16,2304]{2,1,0:T(8,128)S(1)}, f32[2,16,2304]{2,1,0:T(8,128)}, u32[]{:S(2)}) copy-start(f32[2,16,2304]{2,1,0:T(8,128)} %get-tuple-element.483) | copy-start | bytes 884740 | tf_op jit(solution)/shard_map/while
  478.3 0.9 copy-start.4
  (1 other events, 0.8 us)
Sparse Core Ops, SparseCore 0:
  38.2 22.9 reduce-scatter.1
  91.4 21.7 reduce-scatter.1
  143.3 21.7 reduce-scatter.1
  195.4 21.7 reduce-scatter.1
  247.4 21.7 reduce-scatter.1
  299.4 21.7 reduce-scatter.1
  351.4 21.7 reduce-scatter.1
  403.5 21.7 reduce-scatter.1
  455.5 21.7 reduce-scatter.1
where the time goes:
time: 487 us; the launch traced here: 486 us
  waiting for transfers between devices  244 us (50%)
  matrix products  121 us (25%)
  blocking collectives  53.4 us (11%)
  starting transfers between devices  24.8 us (5%)
  other arithmetic  24.6 us (5%)
  between operations  13.8 us (3%)
    reduce_scatter x9, waiting for transfers between devices, advance(): lax.psum_scatter(jnp.dot(grad_latent, encoder.T, preferred_element_type=j...  199 us
    dot_general x9, matrix products, advance(): jnp.dot(got_above, next_weight.T, preferred_element_type=jnp.float32)  60.8 us
    all_gather x9, blocking collectives, advance(): full_upper = lax.all_gather(upper_bf, 'lat', axis=0, tiled=True)  53.4 us
    ppermute x18, waiting for transfers between devices, shifted(): return lax.ppermute(block, axis, route)  45.6 us
    dot_general x9, matrix products, advance(): jnp.dot(grad_latent, encoder.T, preferred_element_type=jnp.float32)  34 us
    dot_general x9, matrix products, advance(): jnp.dot(full_upper, own_weight.T, preferred_element_type=jnp.float32)  26.6 us
    ppermute x18, starting transfers between devices, shifted(): return lax.ppermute(block, axis, route)  24.4 us
  transfers between devices with their start and end apart: 27, of which 18 were waited for; matrix products, arithmetic and copies ran while one was open for 3% of the time, Pallas kernels for 0%

commit v1 on v0

v1 whole, which is shorter than its diff:
```python
import functools

import jax
import jax.numpy as jnp
from jax import lax
from jax.experimental import pallas as pl
from jax.experimental.pallas import tpu as pltpu
from jax.sharding import PartitionSpec as P

MESH = pl.DeviceIdType.MESH
NT_DIMS = (((1,), (1,)), ((), ()))


def pick(total, wanted, unit):
    best = unit
    for size in range(unit, wanted + 1, unit):
        if total % size == 0:
            best = size
    return best


def kernel(
    dims, act_hbm, mask_ref, enc_hbm, own_hbm, next_hbm, seed_ref, grads_ref, attr_ref,
    own_w, next_w, enc_w, act, qbuf, abuf, seedq, qout, lo_out, lo_in, psend, pfull, rsbuf, acc, gl, r_up,
    load_sem, rs_send, rs_recv, q_send, q_recv, a_send, a_recv, lo_send, lo_recv,
    qf_send, qf_recv, af_send, af_recv, iq_send, ia_send,
):
    S, N, C, R, D, LATL, PIECES, LT, ET, LOADS, BW = dims
    half = N // 2
    T = N * R
    DP = D // PIECES
    s = lax.axis_index("section")
    j = lax.axis_index("lat")
    partner = j + 1 - 2 * lax.rem(j, 2)
    top = s == S - 1

    def load(array, k):
        src, dst = ((own_hbm, own_w), (enc_hbm, enc_w), (next_hbm, next_w))[array]
        rows = src.shape[0] // LOADS
        part = pl.ds(k * rows, rows)
        return pltpu.make_async_copy(src.at[part], dst.at[part], load_sem.at[array, k])

    act_load = pltpu.make_async_copy(act_hbm, act, load_sem.at[3, 0])
    for array in range(3):
        for k in range(LOADS):
            load(array, k).start()
        if array == 0:
            act_load.start()

    def remote(src, dst, send, recv, section, lat):
        return pltpu.make_async_remote_copy(
            src_ref=src, dst_ref=dst, send_sem=send, recv_sem=recv, device_id=(section, lat), device_id_type=MESH
        )

    def cols(p):
        return pl.ds(p * DP, DP)

    def mate(k):
        return lax.rem(j + 2 * k, N)

    def block(base, k):
        return lax.rem(base + N - 2 * k, N)

    def q_copy(src, send, c, p, k, section):
        return remote(src.at[c, :, cols(p)], qbuf.at[c, j, :, cols(p)], send.at[c, p, k], q_recv.at[c, p, k], section, mate(k))

    def a_copy(src, send, c, k, section):
        return remote(src.at[c], abuf.at[c, j], send.at[c, k], a_recv.at[c, k], section, mate(k))

    def lo_copy(c):
        return remote(lo_out.at[c], lo_in.at[c], lo_send.at[c], lo_recv.at[c], s - 1, j)

    def rs_copy(c, p, k):
        to = lax.rem(j + k, N)
        return remote(psend.at[c, to, :, cols(p)], rsbuf.at[c, k - 1, :, cols(p)], rs_send.at[c, p, k - 1], rs_recv.at[c, p, k - 1], s, to)

    def qf_copy(c, p, k, base):
        at = qbuf.at[c, block(base, k), :, cols(p)]
        return remote(at, at, qf_send.at[c, p, k], qf_recv.at[c, p, k], s, partner)

    def af_copy(c, k, base):
        at = abuf.at[c, block(base, k)]
        return remote(at, at, af_send.at[c, k], af_recv.at[c, k], s, partner)

    barrier = pltpu.get_barrier_semaphore()
    for k in range(1, N):
        pl.semaphore_signal(barrier, inc=1, device_id=(s, lax.rem(j + k, N)), device_id_type=MESH)
    for step in (1, 2):
        for sign in (step, S - step):
            for k in range(half):
                pl.semaphore_signal(barrier, inc=1, device_id=(lax.rem(s + sign, S), mate(k)), device_id_type=MESH)
    pl.semaphore_wait(barrier, (N - 1) + 4 * half)

    @pl.when(top)
    def _():
        for c in range(C):
            seedq[c] = seed_ref[c].astype(jnp.bfloat16)
            for p in range(PIECES):
                for k in range(1, half):
                    q_copy(seedq, iq_send, c, p, k, s).start()
            qbuf[c, j] = seed_ref[c].astype(jnp.bfloat16)
        for c in range(C):
            for k in range(half):
                a_copy(seedq, ia_send, c, k, s - 1).start()

    def chunk(c, carry):
        @pl.when(top)
        def _():
            acc[...] = jnp.zeros_like(acc)
            r_up[...] = seed_ref[c]

        @pl.when(jnp.logical_not(top))
        def _():
            for k in range(half):
                remote(abuf.at[c, block(j, k)], abuf.at[c, block(j, k)], a_send.at[c, k], a_recv.at[c, k], s, partner).wait_recv()
                af_copy(c, k, j).start()

            @pl.when(c == 0)
            def _():
                for k in range(LOADS):
                    load(2, k).wait()

            for k in range(half):
                af_copy(c, k, partner).wait_recv()

            @pl.loop(0, LATL // LT)
            def _(n):
                rows = pl.ds(pl.multiple_of(n * LT, LT), LT)
                above = abuf[c].reshape(T, D)
                acc[n] = lax.dot_general(above, next_w[rows, :], NT_DIMS, preferred_element_type=jnp.float32)

        @pl.when(c == 0)
        def _():
            for k in range(LOADS):
                load(0, k).wait()
            act_load.wait()

        def arrive(p, k):
            at = qbuf.at[c, block(j, k), :, cols(p)]
            remote(at, at, q_send.at[c, p, k], q_recv.at[c, p, k], s, partner).wait_recv()

        for p in range(PIECES):
            pl.when(jnp.logical_not(top))(functools.partial(arrive, p, 0))
            qf_copy(c, p, 0, j).start()
            for k in range(1, half):
                arrive(p, k)
                qf_copy(c, p, k, j).start()
            for k in range(half):
                qf_copy(c, p, k, partner).wait_recv()

            @pl.loop(0, LATL // LT)
            def _(n):
                rows = pl.ds(pl.multiple_of(n * LT, LT), LT)
                upper = qbuf[c, :, :, cols(p)].reshape(T, DP)
                acc[n] += lax.dot_general(upper, own_w[rows, cols(p)], NT_DIMS, preferred_element_type=jnp.float32)

        @pl.loop(0, LATL // LT)
        def _(n):
            for b in range(LT // BW):
                at = pl.ds(pl.multiple_of(n * LT + b * BW, BW), BW)
                gate = mask_ref[c, n * (LT // BW) + b].astype(jnp.float32)
                grad = acc[n, :, b * BW : (b + 1) * BW]
                active = act[c, :, at].astype(jnp.float32) * gate
                attr_ref[c, :, at] = (active * grad).astype(jnp.bfloat16)
                gl[:, at] = (grad * gate).astype(jnp.bfloat16)

        @pl.when(c == 0)
        def _():
            for k in range(LOADS):
                load(1, k).wait()

        for p in range(PIECES):
            @pl.loop(0, DP // ET)
            def _(n):
                at = pl.ds(pl.multiple_of(p * DP + n * ET, ET), ET)
                part = lax.dot_general(gl[...], enc_w[at, :], NT_DIMS, preferred_element_type=jnp.float32)
                part = part.reshape(N, R, ET)
                pfull[:, :, at] = part
                psend[c, :, :, at] = part.astype(jnp.bfloat16)

            for k in range(1, N):
                rs_copy(c, p, k).start()

        @pl.when(jnp.logical_not(top))
        def _():
            lo_copy(c).wait_recv()
            r_up[...] = qbuf[c, j].astype(jnp.float32) + lo_in[c].astype(jnp.float32)

        for p in range(PIECES):
            total = r_up[:, cols(p)] + pfull[j, :, cols(p)]
            for k in range(1, N):
                rs_copy(c, p, k).wait_recv()
                total += rsbuf[c, k - 1, :, cols(p)].astype(jnp.float32)
            grads_ref[c, :, cols(p)] = total
            rounded = total.astype(jnp.bfloat16)
            qout[c, :, cols(p)] = rounded
            lo_out[c, :, cols(p)] = (total - rounded.astype(jnp.float32)).astype(jnp.bfloat16)

            @pl.when(s >= 1)
            def _():
                for k in range(half):
                    q_copy(qout, q_send, c, p, k, s - 1).start()

        @pl.when(s >= 1)
        def _():
            lo_copy(c).start()

        @pl.when(s >= 2)
        def _():
            for k in range(half):
                a_copy(qout, a_send, c, k, s - 2).start()

        return carry

    lax.fori_loop(0, C, chunk, 0)

    @pl.when(top)
    def _():
        for k in range(LOADS):
            load(2, k).wait()
        for c in range(C):
            for p in range(PIECES):
                for k in range(1, half):
                    q_copy(seedq, iq_send, c, p, k, s).wait_send()
            for k in range(half):
                a_copy(seedq, ia_send, c, k, s - 1).wait_send()

    for c in range(C):
        for p in range(PIECES):
            for k in range(1, N):
                rs_copy(c, p, k).wait_send()
            for k in range(half):
                qf_copy(c, p, k, j).wait_send()

    @pl.when(jnp.logical_not(top))
    def _():
        for c in range(C):
            for k in range(half):
                af_copy(c, k, j).wait_send()

    @pl.when(s >= 1)
    def _():
        for c in range(C):
            for p in range(PIECES):
                for k in range(half):
                    q_copy(qout, q_send, c, p, k, s - 1).wait_send()
            lo_copy(c).wait_send()

    @pl.when(s >= 2)
    def _():
        for c in range(C):
            for k in range(half):
                a_copy(qout, a_send, c, k, s - 2).wait_send()


def solution(mesh):
    S, N = mesh.shape["section"], mesh.shape["lat"]

    def local(activations, block_mask, enc_weight, dec_own, dec_next, grad_seed):
        C, T, LATL = activations.shape[1:]
        R, D = grad_seed.shape[1:]
        BW = LATL // block_mask.shape[2]
        half = N // 2
        DP = pick(D, 768, 128)
        PIECES = D // DP
        LT = pick(LATL, 512, BW)
        ET = pick(DP, 256, 128)
        LOADS = 4
        dims = (S, N, C, R, D, LATL, PIECES, LT, ET, LOADS, BW)
        bf, f32 = jnp.bfloat16, jnp.float32
        dma = pltpu.SemaphoreType.DMA
        vmem = pl.BlockSpec(memory_space=pltpu.VMEM)
        smem = pl.BlockSpec(memory_space=pltpu.SMEM)
        hbm = pl.BlockSpec(memory_space=pl.ANY)
        grads, attribution = pl.pallas_call(
            functools.partial(kernel, dims),
            out_shape=(jax.ShapeDtypeStruct((C, R, D), f32), jax.ShapeDtypeStruct((C, T, LATL), bf)),
            in_specs=[hbm, smem, hbm, hbm, hbm, vmem],
            out_specs=(vmem, vmem),
            scratch_shapes=[
                pltpu.VMEM((LATL, D), bf),
                pltpu.VMEM((LATL, D), bf),
                pltpu.VMEM((D, LATL), bf),
                pltpu.VMEM((C, T, LATL), bf),
                pltpu.VMEM((C, N, R, D), bf),
                pltpu.VMEM((C, N, R, D), bf),
                pltpu.VMEM((C, R, D), bf),
                pltpu.VMEM((C, R, D), bf),
                pltpu.VMEM((C, R, D), bf),
                pltpu.VMEM((C, R, D), bf),
                pltpu.VMEM((C, N, R, D), bf),
                pltpu.VMEM((N, R, D), f32),
                pltpu.VMEM((C, N - 1, R, D), bf),
                pltpu.VMEM((LATL // LT, T, LT), f32),
                pltpu.VMEM((T, LATL), bf),
                pltpu.VMEM((R, D), f32),
                dma((4, LOADS)),
                dma((C, PIECES, N - 1)),
                dma((C, PIECES, N - 1)),
                dma((C, PIECES, half)),
                dma((C, PIECES, half)),
                dma((C, half)),
                dma((C, half)),
                dma((C,)),
                dma((C,)),
                dma((C, PIECES, half)),
                dma((C, PIECES, half)),
                dma((C, half)),
                dma((C, half)),
                dma((C, PIECES, half)),
                dma((C, half)),
            ],
            compiler_params=pltpu.CompilerParams(
                collective_id=0, has_side_effects=True, vmem_limit_bytes=56 * 1024 * 1024
            ),
        )(activations[0], block_mask[0], enc_weight[0], dec_own[0], dec_next[0], grad_seed)
        return grads[None], attribution[None]

    placed = (
        P("section", None, None, "lat"),
        P("section", None, "lat"),
        P("section", None, "lat"),
        P("section", "lat", None),
        P("section", "lat", None),
        P(None, "lat", None),
    )
    return jax.shard_map(
        local,
        mesh=mesh,
        in_specs=placed,
        out_specs=(P("section", None, "lat", None), P("section", None, None, "lat")),
        check_vma=False,
    )
```

time: 487 us -> 158 us (0.32)
  waiting for transfers between devices: 244 us -> 0 us
  Pallas kernels: 0 us -> 153 us
  matrix products: 121 us -> 0 us
  blocking collectives: 53.4 us -> 0 us
  starting transfers between devices: 24.8 us -> 0 us
  other arithmetic: 24.6 us -> 0 us
  between operations: 13.8 us -> 0.64 us
    reduce_scatter x9 -> x0, waiting for transfers between devices: 199 us -> none  [advance(): lax.psum_scatter(jnp.dot(grad_latent, encoder.T, preferred_element_type=j...]
    pallas_call x0 -> x1, Pallas kernels: none -> 153 us  [local(): pl.pallas_call(functools.partial(kernel, dims), out_shape=(jax.ShapeDtype...]
    dot_general x27 -> x0, matrix products: 121 us -> none  [the longest x9 60.8 us: advance(): jnp.dot(got_above, next_weight.T, preferred_element_type=jnp.float32)]
    all_gather x9 -> x0, blocking collectives: 53.4 us -> none  [advance(): full_upper = lax.all_gather(upper_bf, 'lat', axis=0, tiled=True)]
    ppermute x18 -> x0, waiting for transfers between devices: 45.6 us -> none  [shifted(): return lax.ppermute(block, axis, route)]
    ppermute x18 -> x0, starting transfers between devices: 24.4 us -> none  [shifted(): return lax.ppermute(block, axis, route)]
    convert_element_type x18 -> x0, other arithmetic: 15.9 us -> none  [the longest x9 8.34 us: advance(): upper_bf = grad_upper.astype(jnp.bfloat16)]
    select_n x9 -> x0, other arithmetic: 8.54 us -> none  [advance(): grads_acc = jnp.where(is_valid, grads_new, grads_acc)]
  transfers between devices with their start and end apart: 27 -> 0, of which waited for: 18 -> 0; matrix products, arithmetic and copies ran while one was open for 3% -> 0% of each run, Pallas kernels for 0% -> 0%
where the time goes in v1:
time: 158 us; the launch traced here: 157 us
  Pallas kernels  153 us (97%)
  local copies, waits for them, and re-layouts  3.58 us (2%)
    pallas_call x1, Pallas kernels, local(): pl.pallas_call(functools.partial(kernel, dims), out_shape=(jax.ShapeDtype...  153 us
    unnamed x2, local copies, waits for them, and re-layouts  3.58 us

profile of v1, /device:TPU:0, one launch (start us, length us, event | category | flops | bytes accessed | tf_op | source)
XLA Modules:
  0.0 157.4 jit_solution(3832154711126498608)
XLA Ops:
  0.6 153.2 %shard_map.77 = (f32[2,16,2304]{2,1,0:T(8,128)}, bf16[2,64,2048]{2,1,0:T(8,128)(2,1)}) custom-call(bf16[2,64,2048]{2,1,0:T(8,128)(2,1)} %bitcast.10, s32[2,16]{1,0:T(2,128)} %bitcast.13, bf16[2304,2048]{1,0:T(8,128)(2,1)} %bitcast.7, bf16[2048,2304]{1,0:T(8,128)(2,1)} %bitcast.8, bf16[2048,2304]{1,0:T(8,128)(2,1)} %bitcast.9, f32[2,16,2304]{2,1,0:T(8,128)} %seed_ref.1), custom_call_target="tpu_custom_call" | custom-call | tf_op jit(solution)/shard_map/pallas_call | solution.py:275
  153.8 1.7 %copy.10 = f32[1,2,16,2304]{3,2,1,0:T(8,128)} copy(f32[1,2,16,2304]{3,2,1,0:T(8,128)} %bitcast.12) | data formatting | bytes 589824
  155.5 1.9 %copy.11 = bf16[1,2,64,2048]{3,2,1,0:T(8,128)(2,1)} copy(bf16[1,2,64,2048]{3,2,1,0:T(8,128)(2,1)} %bitcast.11) | data formatting | bytes 1048576

commit v2 on v1

--- a/solution.py
+++ b/solution.py
@@ -9,6 +9,7 @@
 
 MESH = pl.DeviceIdType.MESH
 NT_DIMS = (((1,), (1,)), ((), ()))
+NN_DIMS = (((1,), (0,)), ((), ()))
 
 
 def pick(total, wanted, unit):
@@ -21,11 +22,11 @@
 
 def kernel(
     dims, act_hbm, mask_ref, enc_hbm, own_hbm, next_hbm, seed_ref, grads_ref, attr_ref,
-    own_w, next_w, enc_w, act, qbuf, abuf, seedq, qout, lo_out, lo_in, psend, pfull, rsbuf, acc, gl, r_up,
+    own_w, next_w, enc_w, own_t, enc_t, act, qbuf, abuf, seedq, qout, lo_out, lo_in, psend, pfull, rsbuf, acc, gl, r_up,
     load_sem, rs_send, rs_recv, q_send, q_recv, a_send, a_recv, lo_send, lo_recv,
     qf_send, qf_recv, af_send, af_recv, iq_send, ia_send,
 ):
-    S, N, C, R, D, LATL, PIECES, LT, ET, LOADS, BW = dims
+    S, N, C, R, D, LATL, PIECES, LT, ET, TB, LOADS, BW = dims
     half = N // 2
     T = N * R
     DP = D // PIECES
@@ -103,6 +104,28 @@
             for k in range(half):
                 a_copy(seedq, ia_send, c, k, s - 1).start()
 
+    @pl.when(jnp.logical_not(top))
+    def _():
+        for k in range(LOADS):
+            load(0, k).wait()
+
+        @pl.loop(0, LATL // LT)
+        def _(n):
+            @pl.loop(0, D // TB)
+            def _(d):
+                at = pl.ds(pl.multiple_of(d * TB, TB), TB)
+                own_t[n, at, :] = own_w[pl.ds(pl.multiple_of(n * LT, LT), LT), at].T
+
+        for k in range(LOADS):
+            load(1, k).wait()
+
+        @pl.loop(0, D // ET)
+        def _(e):
+            @pl.loop(0, LATL // TB)
+            def _(n):
+                at = pl.ds(pl.multiple_of(n * TB, TB), TB)
+                enc_t[e, at, :] = enc_w[pl.ds(pl.multiple_of(e * ET, ET), ET), at].T
+
     def chunk(c, carry):
         @pl.when(top)
         def _():
@@ -129,11 +152,10 @@
                 above = abuf[c].reshape(T, D)
                 acc[n] = lax.dot_general(above, next_w[rows, :], NT_DIMS, preferred_element_type=jnp.float32)
 
-        @pl.when(c == 0)
+        @pl.when(jnp.logical_and(top, c == 0))
         def _():
             for k in range(LOADS):
                 load(0, k).wait()
-            act_load.wait()
 
         def arrive(p, k):
             at = qbuf.at[c, block(j, k), :, cols(p)]
@@ -152,7 +174,14 @@
             def _(n):
                 rows = pl.ds(pl.multiple_of(n * LT, LT), LT)
                 upper = qbuf[c, :, :, cols(p)].reshape(T, DP)
-                acc[n] += lax.dot_general(upper, own_w[rows, cols(p)], NT_DIMS, preferred_element_type=jnp.float32)
+
+                @pl.when(top)
+                def _():
+                    acc[n] += lax.dot_general(upper, own_w[rows, cols(p)], NT_DIMS, preferred_element_type=jnp.float32)
+
+                @pl.when(jnp.logical_not(top))
+                def _():
+                    acc[n] += lax.dot_general(upper, own_t[n, cols(p), :], NN_DIMS, preferred_element_type=jnp.float32)
 
         @pl.loop(0, LATL // LT)
         def _(n):
@@ -160,11 +189,9 @@
                 at = pl.ds(pl.multiple_of(n * LT + b * BW, BW), BW)
                 gate = mask_ref[c, n * (LT // BW) + b].astype(jnp.float32)
                 grad = acc[n, :, b * BW : (b + 1) * BW]
-                active = act[c, :, at].astype(jnp.float32) * gate
-                attr_ref[c, :, at] = (active * grad).astype(jnp.bfloat16)
                 gl[:, at] = (grad * gate).astype(jnp.bfloat16)
 
-        @pl.when(c == 0)
+        @pl.when(jnp.logical_and(top, c == 0))
         def _():
             for k in range(LOADS):
                 load(1, k).wait()
@@ -173,13 +200,34 @@
             @pl.loop(0, DP // ET)
             def _(n):
                 at = pl.ds(pl.multiple_of(p * DP + n * ET, ET), ET)
-                part = lax.dot_general(gl[...], enc_w[at, :], NT_DIMS, preferred_element_type=jnp.float32)
-                part = part.reshape(N, R, ET)
-                pfull[:, :, at] = part
-                psend[c, :, :, at] = part.astype(jnp.bfloat16)
+                def keep(part):
+                    part = part.reshape(N, R, ET)
+                    pfull[:, :, at] = part
+                    psend[c, :, :, at] = part.astype(jnp.bfloat16)
+
+                @pl.when(top)
+                def _():
+                    keep(lax.dot_general(gl[...], enc_w[at, :], NT_DIMS, preferred_element_type=jnp.float32))
+
+                @pl.when(jnp.logical_not(top))
+                def _():
+                    e = p * (DP // ET) + n
+                    keep(lax.dot_general(gl[...], enc_t[e], NN_DIMS, preferred_element_type=jnp.float32))
 
             for k in range(1, N):
                 rs_copy(c, p, k).start()
+
+        @pl.when(c == 0)
+        def _():
+            act_load.wait()
+
+        @pl.loop(0, LATL // LT)
+        def _(n):
+            for b in range(LT // BW):
+                at = pl.ds(pl.multiple_of(n * LT + b * BW, BW), BW)
+                gate = mask_ref[c, n * (LT // BW) + b].astype(jnp.float32)
+                active = act[c, :, at].astype(jnp.float32) * gate
+                attr_ref[c, :, at] = (active * acc[n, :, b * BW : (b + 1) * BW]).astype(jnp.bfloat16)
 
         @pl.when(jnp.logical_not(top))
         def _():
@@ -191,15 +239,16 @@
             for k in range(1, N):
                 rs_copy(c, p, k).wait_recv()
                 total += rsbuf[c, k - 1, :, cols(p)].astype(jnp.float32)
-            grads_ref[c, :, cols(p)] = total
             rounded = total.astype(jnp.bfloat16)
             qout[c, :, cols(p)] = rounded
-            lo_out[c, :, cols(p)] = (total - rounded.astype(jnp.float32)).astype(jnp.bfloat16)
 
             @pl.when(s >= 1)
             def _():
-                for k in range(half):
+                for k in reversed(range(half)):
                     q_copy(qout, q_send, c, p, k, s - 1).start()
+
+            grads_ref[c, :, cols(p)] = total
+            lo_out[c, :, cols(p)] = (total - rounded.astype(jnp.float32)).astype(jnp.bfloat16)
 
         @pl.when(s >= 1)
         def _():
@@ -261,12 +310,13 @@
         R, D = grad_seed.shape[1:]
         BW = LATL // block_mask.shape[2]
         half = N // 2
-        DP = pick(D, 768, 128)
+        DP = pick(D, 1152, 128)
         PIECES = D // DP
-        LT = pick(LATL, 512, BW)
-        ET = pick(DP, 256, 128)
+        LT = pick(LATL, 2048, BW)
+        ET = pick(DP, 1152, 128)
+        TB = 256 if D % 256 == 0 and LATL % 256 == 0 else 128
         LOADS = 4
-        dims = (S, N, C, R, D, LATL, PIECES, LT, ET, LOADS, BW)
+        dims = (S, N, C, R, D, LATL, PIECES, LT, ET, TB, LOADS, BW)
         bf, f32 = jnp.bfloat16, jnp.float32
         dma = pltpu.SemaphoreType.DMA
         vmem = pl.BlockSpec(memory_space=pltpu.VMEM)
@@ -281,6 +331,8 @@
                 pltpu.VMEM((LATL, D), bf),
                 pltpu.VMEM((LATL, D), bf),
                 pltpu.VMEM((D, LATL), bf),
+                pltpu.VMEM((LATL // LT, D, LT), bf),
+                pltpu.VMEM((D // ET, LATL, ET), bf),
                 pltpu.VMEM((C, T, LATL), bf),
                 pltpu.VMEM((C, N, R, D), bf),
                 pltpu.VMEM((C, N, R, D), bf),

time: 158 us -> 131 us (0.83)
  Pallas kernels: 153 us -> 127 us
    pallas_call x1, Pallas kernels: 153 us -> 127 us  [local(): pl.pallas_call(functools.partial(kernel, dims), out_shape=(jax.ShapeDtype...]
where the time goes in v2:
time: 131 us
  Pallas kernels  127 us (97%)
  local copies, waits for them, and re-layouts  3.58 us (3%)
    pallas_call x1, Pallas kernels, local(): pl.pallas_call(functools.partial(kernel, dims), out_shape=(jax.ShapeDtype...  127 us
    unnamed x2, local copies, waits for them, and re-layouts  3.58 us

profile of v2, /device:TPU:0, one launch (start us, length us, event | category | flops | bytes accessed | tf_op | source)
XLA Modules:
  0.0 131.0 jit_solution(14591592443768578091)
XLA Ops:
  0.6 126.7 %shard_map.77 = (f32[2,16,2304]{2,1,0:T(8,128)}, bf16[2,64,2048]{2,1,0:T(8,128)(2,1)}) custom-call(bf16[2,64,2048]{2,1,0:T(8,128)(2,1)} %bitcast.10, s32[2,16]{1,0:T(2,128)} %bitcast.13, bf16[2304,2048]{1,0:T(8,128)(2,1)} %bitcast.7, bf16[2048,2304]{1,0:T(8,128)(2,1)} %bitcast.8, bf16[2048,2304]{1,0:T(8,128)(2,1)} %bitcast.9, f32[2,16,2304]{2,1,0:T(8,128)} %seed_ref.1), custom_call_target="tpu_custom_call" | custom-call | tf_op jit(solution)/shard_map/pallas_call | solution.py:325
  127.4 1.7 %copy.10 = f32[1,2,16,2304]{3,2,1,0:T(8,128)} copy(f32[1,2,16,2304]{3,2,1,0:T(8,128)} %bitcast.12) | data formatting | bytes 589824
  129.1 1.9 %copy.11 = bf16[1,2,64,2048]{3,2,1,0:T(8,128)(2,1)} copy(bf16[1,2,64,2048]{3,2,1,0:T(8,128)(2,1)} %bitcast.11) | data formatting | bytes 1048576
